TPU v7x, 32 devices: a whole 2x2x4 slice. The times are simulated.
32 devices in a mesh: wide: 4 (over y, x), grp: 8 (over z, core).
Axes of the slice: x: 2, y: 2, z: 4, core: 2. Of those that a mesh axis runs over, the one named last changes fastest.
Arguments:
- surf_depth: int32 [4, 8, 8, 4096], P('wide', 'grp'), may hold values from 0 to 1073741823
- surf_color: bfloat16 [4, 8, 8, 3, 4096], P('wide', 'grp'), may hold values from 0 to 2
- surf_box: int32 [4, 8, 8, 4], P('wide', 'grp'), may hold values from 0 to 64, as said below
- vol_color: bfloat16 [4, 8, 4, 8, 3, 4096], P('wide', 'grp'), may hold values from 0 to 4
- vol_alpha: bfloat16 [4, 8, 4, 8, 4096], P('wide', 'grp'), may hold values from 0.0009994507 to 0.039794922
- vol_box: int32 [4, 8, 4, 4], P('wide', 'grp'), may hold values from 0 to 64, as said below
- ray_entry: int32 [4, 8, 4, 4096], P('wide', 'grp'), may hold values from 0 to 939524095
- ray_step: int32 [4, 8, 4, 4096], P('wide', 'grp'), may hold values from 1048576 to 16777215
- order: int32 [8, 4], P('grp'), may hold values from 0 to 3, each once within a row
Outputs:
- frame: float32 [8, 4, 4, 4096], P('grp', 'wide')
Inputs may be any that keep to these rules, and one draw needn't show every extreme that they name: `surf_box`: each box gives rows [top, bottom) and columns [left, right) of a tile with 1 to 16 rows and 1 or more columns; in every draw one tile row has boxes of exactly 16 rows from every source, and other tiles reach it too. `vol_box`: each box gives rows [top, bottom) and columns [left, right) of a tile with 1 to 32 rows and 1 or more columns; in every draw one tile column has boxes of exactly 32 rows from every brick of every band, and other tiles reach it too. `order`: each row is a permutation of 0 .. 3.
All inputs are finite; a program needn't handle non-finite values.
Results may differ from a plain program's by a relative error of at most 0.0003.
Values may be sent and summed in bfloat16 or wider, within the bound.
A program may use at most 64 MiB of HBM per device.

v0:
```python
import jax
import jax.numpy as jnp
from jax import lax
from jax.sharding import PartitionSpec as P

TILE_H = 64
TILE_W = 64


far_depth = 1073741824


def window_mask(box, start, rows, tile_w):
    row_ids = start[..., None, None] + jnp.arange(rows, dtype=jnp.int32)[:, None]
    col_ids = jnp.arange(tile_w, dtype=jnp.int32)[None, :]
    inside = (row_ids >= box[..., 0, None, None]) & (row_ids < box[..., 1, None, None])
    inside = inside & (col_ids >= box[..., 2, None, None]) & (col_ids < box[..., 3, None, None])
    return inside.reshape(box.shape[:-1] + (rows * tile_w,))


def fetch_limit(nearest):
    band_limit = lax.all_gather(nearest[None, :], "wide", axis=0, tiled=True)
    return band_limit


def per_device(
    surf_depth, surf_color, surf_box, vol_color, vol_alpha, vol_box, ray_entry, ray_step, order
):
    tile_pix = TILE_H * TILE_W
    depth = surf_depth[0, 0]
    color = surf_color[0, 0]
    sbox = surf_box[0, 0]
    s_inside = window_mask(sbox, jnp.zeros_like(sbox[:, 0]), TILE_H, TILE_W)
    send_depth = jnp.where(s_inside, depth, far_depth)
    send_color = jnp.where(s_inside[:, None, :], color, jnp.zeros((), jnp.bfloat16))
    frag_depth = lax.all_to_all(send_depth, "grp", split_axis=0, concat_axis=0, tiled=True)
    frag_color = lax.all_to_all(send_color, "grp", split_axis=0, concat_axis=0, tiled=True)
    nearest = jnp.min(frag_depth, axis=0)
    winner = jnp.argmin(frag_depth, axis=0)
    pick = (jnp.arange(frag_depth.shape[0], dtype=jnp.int32)[:, None] == winner[None, :]) & (
        frag_depth < far_depth
    )
    surface = jnp.sum(jnp.where(pick[:, None, :], frag_color.astype(jnp.float32), 0.0), axis=0)
    vcolor = vol_color[0, 0]
    valpha = vol_alpha[0, 0]
    vbox = vol_box[0, 0]
    entry = ray_entry[0, 0]
    stride = ray_step[0, 0]
    v_inside = window_mask(vbox, jnp.zeros_like(vbox[:, 0]), TILE_H, TILE_W)
    samples = valpha.shape[1]
    accum = jnp.zeros((valpha.shape[0], 3, valpha.shape[2]), jnp.float32)
    trans = jnp.ones((valpha.shape[0], valpha.shape[2]), jnp.float32)
    limit = fetch_limit(nearest)
    for k in range(samples):
        kept = v_inside & (entry + k * stride < limit)
        opacity = valpha[:, k].astype(jnp.float32)
        weight = jnp.where(kept, trans * opacity, 0.0)
        accum = accum + weight[:, None, :] * vcolor[:, k].astype(jnp.float32)
        trans = trans * (1.0 - jnp.where(kept, opacity, 0.0))
    layer_accum, layer_trans = (
        lax.all_to_all(accum, "wide", split_axis=0, concat_axis=0, tiled=True),
        lax.all_to_all(trans, "wide", split_axis=0, concat_axis=0, tiled=True),
    )
    rank = order[0]
    ordered_accum = jnp.take(layer_accum, rank, axis=0)
    ordered_trans = jnp.take(layer_trans, rank, axis=0)

    def over(carry, layer):
        color_sum, through = carry
        return ((color_sum + through[None, :] * layer[0], through * layer[1]), None)

    start = (jnp.zeros((3, tile_pix), jnp.float32), jnp.ones((tile_pix,), jnp.float32))
    (color_sum, through), unused = lax.scan(over, start, (ordered_accum, ordered_trans))
    rgb = color_sum + through[None, :] * surface
    frame = jnp.concatenate([rgb, through[None, :]], axis=0)
    return frame[None, None]


def solution(mesh):
    return jax.shard_map(
        per_device,
        mesh=mesh,
        in_specs=(
            P("wide", "grp", None, None),
            P("wide", "grp", None, None, None),
            P("wide", "grp", None, None),
            P("wide", "grp", None, None, None, None),
            P("wide", "grp", None, None, None),
            P("wide", "grp", None, None),
            P("wide", "grp", None, None),
            P("wide", "grp", None, None),
            P("grp", None),
        ),
        out_specs=P("grp", "wide", None, None),
        check_vma=False,
    )
```

profile of v0, /device:TPU:0, one launch (start us, length us, event | category | flops | bytes accessed | tf_op | source)
XLA Modules:
  0.0 57.7 jit_solution(4512932884291679959)
XLA Ops:
  0.0 0.8 %slice_bitcast_fusion.19 = (s32[8]{0:T(128)S(1)}, s32[8]{0:T(128)S(1)}, s32[8]{0:T(128)S(1)}, s32[8]{0:T(128)S(1)}) fusion(s32[8,4]{0,1:T(4,128)} %bitcast.261), kind=kLoop, calls=%fused_computation.140 | loop fusion | bytes 256 | tf_op jit(solution)/shard_map/slice | solution.py:16
  1.0 0.1 and_and_fusion
  1.1 0.2 and.147
  1.4 0.8 %copy.43 = s32[8,1,4096]{2,1,0:T(1,128)} copy(s32[8,1,4096]{2,0,1:T(8,128)S(1)} %bitcast_select_fusion.1) | data formatting | bytes 262144 | tf_op jit(solution)/shard_map/jit(_where)/select_n | solution.py:34
  2.2 6.5 %all-to-all-start = ((s32[8,1,4096]{2,1,0:T(1,128)}), s32[8,1,4096]{2,1,0:T(1,128)S(1)}, u32[]{:S(2)}, u32[]{:S(2)}) async-start(s32[8,1,4096]{2,1,0:T(1,128)} %copy.43), calls=%async_computation | async-start | bytes 262144 | tf_op jit(solution)/shard_map/all_to_all | solution.py:36
  8.7 0.2 and.157
  8.9 0.2 slice_reduce_fusion.3
  9.2 1.0 %bitcast_select_fusion = bf16[8,3,4096]{2,1,0:T(4,128)(2,1)} fusion(bf16[1,1,8,3,4096]{4,2,3,1,0:T(8,128)(2,1)S(1)} %copy-done.2, pred[8,4096]{1,0:T(8,128)(4,1)S(1)} %and.157), kind=kLoop, calls=%fused_computation.8 | loop fusion | flops 98304 | bytes 425984 | tf_op jit(solution)/shard_map/jit(_where)/select_n | solution.py:35
  10.5 0.2 copy.58
  10.7 0.6 %copy.57 = bf16[1,1,4,8,3,4096]{5,2,4,3,1,0:T(4,128)(2,1)S(1)} copy(bf16[1,1,4,8,3,4096]{5,3,4,2,1,0:T(8,128)(2,1)S(1)} %copy-done) | data formatting | bytes 1572864 | tf_op args[3]
  11.4 4.1 %all-to-all-done = s32[8,1,4096]{2,1,0:T(1,128)S(1)} async-done(((s32[8,1,4096]{2,1,0:T(1,128)}), s32[8,1,4096]{2,1,0:T(1,128)S(1)}, u32[]{:S(2)}, u32[]{:S(2)}) %all-to-all-start) | async-done | bytes 131104 | tf_op jit(solution)/shard_map/all_to_all | solution.py:36
  15.4 0.1 reduce_min.9
  15.6 8.2 %all-gather = s32[16384]{0:T(1024)S(1)} all-gather(s32[4096]{0:T(1024)S(1)} %reduce_min.9), channel_id=2, replica_groups=mesh['wide'=4,'grp'=8] {'wide'}, dimensions={0}, use_global_device_ids=true | all-gather | bytes 81920 | tf_op jit(solution)/shard_map/all_gather | solution.py:22
  23.9 0.8 %copy-done.4 = s32[1,1,4,4096]{3,2,1,0:T(4,128)S(1)} copy-done((s32[1,1,4,4096]{3,2,1,0:T(4,128)S(1)}, s32[1,1,4,4096]{3,2,1,0:T(4,128)}, u32[]{:S(2)}) %copy-start.4) | copy-done | bytes 65560
  24.7 0.4 fusion.30
  25.1 0.7 %all_to_all.22 = f32[4,1,4096]{2,1,0:T(1,128)} reshape(f32[4,4096]{1,0:T(4,128)S(1)} %get-tuple-element.76) | data formatting | bytes 131072 | tf_op jit(solution)/shard_map/all_to_all | solution.py:62
  25.8 3.3 %all-to-all-start.2 = ((f32[4,1,4096]{2,1,0:T(1,128)}), f32[4,1,4096]{2,1,0:T(1,128)S(1)}, u32[]{:S(2)}, u32[]{:S(2)}) async-start(f32[4,1,4096]{2,1,0:T(1,128)} %all_to_all.22), calls=%async_computation.2 | async-start | bytes 131072 | tf_op jit(solution)/shard_map/all_to_all | solution.py:62
  29.1 0.2 fusion.13
  29.3 0.3 fusion.1
  29.6 0.8 %bitcast_reduce_fusion = (s32[4096]{0:T(1024)}, s32[4096]{0:T(1024)S(1)}) fusion(s32[8,1,4096]{2,1,0:T(1,128)S(1)} %all-to-all-done), kind=kLoop, calls=%fused_computation.26 | loop fusion | flops 200704 | bytes 163840 | tf_op jit(solution)/shard_map/per_device/reduce | solution.py:39
  30.4 3.4 %all-to-all-done.2 = f32[4,1,4096]{2,1,0:T(1,128)S(1)} async-done(((f32[4,1,4096]{2,1,0:T(1,128)}), f32[4,1,4096]{2,1,0:T(1,128)S(1)}, u32[]{:S(2)}, u32[]{:S(2)}) %all-to-all-start.2) | async-done | bytes 65568 | tf_op jit(solution)/shard_map/all_to_all | solution.py:62
  33.9 3.4 %all-to-all-start.3 = ((bf16[8,3,4096]{2,1,0:T(4,128)(2,1)}), bf16[8,3,4096]{2,1,0:T(4,128)(2,1)S(1)}, u32[]{:S(2)}, u32[]{:S(2)}) async-start(bf16[8,3,4096]{2,1,0:T(4,128)(2,1)} %bitcast_select_fusion), calls=%async_computation.3 | async-start | bytes 524288 | tf_op jit(solution)/shard_map/all_to_all | solution.py:37
  37.4 0.8 %copy.46 = f32[4,3,4096]{2,1,0:T(4,128)} copy(f32[4,3,4096]{2,0,1:T(4,128)S(1)} %fusion.1) | data formatting | bytes 393216 | tf_op jit(solution)/shard_map/add | solution.py:58
  38.3 0.6 %gather_fusion.1 = f32[4,4096]{1,0:T(4,128)S(1)} fusion(f32[4,4096]{1,0:T(4,128)S(1)} %bitcast.253, s32[1024]{0:T(1024)S(1)} %pad_clamp_fusion), kind=kCustom, calls=%fused_computation.1 | custom fusion | bytes 131088 | tf_op jit(solution)/shard_map/jit(_take)/gather | solution.py:66
  38.9 8.1 %all-to-all-done.3 = bf16[8,3,4096]{2,1,0:T(4,128)(2,1)S(1)} async-done(((bf16[8,3,4096]{2,1,0:T(4,128)(2,1)}), bf16[8,3,4096]{2,1,0:T(4,128)(2,1)S(1)}, u32[]{:S(2)}, u32[]{:S(2)}) %all-to-all-start.3) | async-done | bytes 196640 | tf_op jit(solution)/shard_map/all_to_all | solution.py:37
  46.9 3.4 %all-to-all-start.1 = ((f32[4,3,4096]{2,1,0:T(4,128)}), f32[4,3,4096]{2,1,0:T(4,128)S(1)}, u32[]{:S(2)}, u32[]{:S(2)}) async-start(f32[4,3,4096]{2,1,0:T(4,128)} %copy.46), calls=%async_computation.1 | async-start | bytes 524288 | tf_op jit(solution)/shard_map/all_to_all | solution.py:61
  50.4 0.2 select_reduce_fusion
  50.6 5.0 %all-to-all-done.1 = f32[4,3,4096]{2,1,0:T(4,128)S(1)} async-done(((f32[4,3,4096]{2,1,0:T(4,128)}), f32[4,3,4096]{2,1,0:T(4,128)S(1)}, u32[]{:S(2)}, u32[]{:S(2)}) %all-to-all-start.1) | async-done | bytes 196640 | tf_op jit(solution)/shard_map/all_to_all | solution.py:61
  55.7 0.7 %gather_fusion = f32[4,3,4096]{2,1,0:T(4,128)S(1)} fusion(f32[4,3,4096]{2,1,0:T(4,128)S(1)} %all-to-all-done.1, s32[1024]{0:T(1024)S(1)} %pad_clamp_fusion), kind=kCustom, calls=%fused_computation | custom fusion | bytes 393232 | tf_op jit(solution)/shard_map/jit(_take)/gather | solution.py:65
  56.4 0.1 broadcast_select_fusion.1
  56.5 0.5 while.13
  57.1 0.7 %maximum_bitcast_fusion = f32[1,1,4,4096]{3,2,1,0:T(4,128)} fusion(f32[1,4096]{1,0:T(1,128)S(1)} %bitcast.259, f32[3,4096]{1,0:T(4,128)S(1)} %multiply_add_fusion), kind=kLoop, calls=%fused_computation.76 | loop fusion | flops 16384 | bytes 131072 | tf_op jit(solution)/shard_map/broadcast_in_dim | solution.py:76
  (45 shorter events, 1.4 us)
Async XLA Ops:
  0.0 1.3 %copy-start.3 = (s32[1,1,8,4096]{3,2,1,0:T(8,128)S(1)}, s32[1,1,8,4096]{3,2,1,0:T(8,128)}, u32[]{:S(2)}) copy-start(s32[1,1,8,4096]{3,2,1,0:T(8,128)} %param.11) | copy-start | bytes 393220
  1.3 7.5 %copy-start.7 = (s32[1,4]{1,0:T(1,128)S(1)}, s32[1,4]{1,0:T(1,128)}, u32[]{:S(2)}) copy-start(s32[1,4]{1,0:T(1,128)} %param.19) | copy-start | bytes 52
  1.4 7.5 %copy-start.6 = (s32[1,1,4,4]{3,2,1,0:T(4,128)S(1)}, s32[1,1,4,4]{3,2,1,0:T(4,128)}, u32[]{:S(2)}) copy-start(s32[1,1,4,4]{3,2,1,0:T(4,128)} %param.16) | copy-start | bytes 196
  1.4 7.9 %copy-start.2 = (bf16[1,1,8,3,4096]{4,2,3,1,0:T(8,128)(2,1)S(1)}, bf16[1,1,8,3,4096]{4,2,3,1,0:T(8,128)(2,1)}, u32[]{:S(2)}) copy-start(bf16[1,1,8,3,4096]{4,2,3,1,0:T(8,128)(2,1)} %param.12) | copy-start | bytes 589828
  1.4 9.1 %copy-start.1 = (bf16[1,1,4,8,4096]{4,3,2,1,0:T(8,128)(2,1)S(1)}, bf16[1,1,4,8,4096]{4,3,2,1,0:T(8,128)(2,1)}, u32[]{:S(2)}) copy-start(bf16[1,1,4,8,4096]{4,3,2,1,0:T(8,128)(2,1)} %param.15) | copy-start | bytes 786436
  2.2 8.5 %copy-start = (bf16[1,1,4,8,3,4096]{5,3,4,2,1,0:T(8,128)(2,1)S(1)}, bf16[1,1,4,8,3,4096]{5,3,4,2,1,0:T(8,128)(2,1)}, u32[]{:S(2)}) copy-start(bf16[1,1,4,8,3,4096]{5,3,4,2,1,0:T(8,128)(2,1)} %param.14) | copy-start | bytes 2359300
  2.2 13.2 %all-to-all-start = ((s32[8,1,4096]{2,1,0:T(1,128)}), s32[8,1,4096]{2,1,0:T(1,128)S(1)}, u32[]{:S(2)}, u32[]{:S(2)}) async-start(s32[8,1,4096]{2,1,0:T(1,128)} %copy.43), calls=%async_computation | async-start | bytes 262144 | tf_op jit(solution)/shard_map/all_to_all | solution.py:36
  23.8 0.8 %copy-start.4 = (s32[1,1,4,4096]{3,2,1,0:T(4,128)S(1)}, s32[1,1,4,4096]{3,2,1,0:T(4,128)}, u32[]{:S(2)}) copy-start(s32[1,1,4,4096]{3,2,1,0:T(4,128)} %param.18) | copy-start | bytes 196612
  23.8 0.9 %copy-start.5 = (s32[1,1,4,4096]{3,2,1,0:T(4,128)S(1)}, s32[1,1,4,4096]{3,2,1,0:T(4,128)}, u32[]{:S(2)}) copy-start(s32[1,1,4,4096]{3,2,1,0:T(4,128)} %param.17) | copy-start | bytes 196612
  25.8 8.1 %all-to-all-start.2 = ((f32[4,1,4096]{2,1,0:T(1,128)}), f32[4,1,4096]{2,1,0:T(1,128)S(1)}, u32[]{:S(2)}, u32[]{:S(2)}) async-start(f32[4,1,4096]{2,1,0:T(1,128)} %all_to_all.22), calls=%async_computation.2 | async-start | bytes 131072 | tf_op jit(solution)/shard_map/all_to_all | solution.py:62
  33.9 13.1 %all-to-all-start.3 = ((bf16[8,3,4096]{2,1,0:T(4,128)(2,1)}), bf16[8,3,4096]{2,1,0:T(4,128)(2,1)S(1)}, u32[]{:S(2)}, u32[]{:S(2)}) async-start(bf16[8,3,4096]{2,1,0:T(4,128)(2,1)} %bitcast_select_fusion), calls=%async_computation.3 | async-start | bytes 524288 | tf_op jit(solution)/shard_map/all_to_all | solution.py:37
  46.9 8.8 %all-to-all-start.1 = ((f32[4,3,4096]{2,1,0:T(4,128)}), f32[4,3,4096]{2,1,0:T(4,128)S(1)}, u32[]{:S(2)}, u32[]{:S(2)}) async-start(f32[4,3,4096]{2,1,0:T(4,128)} %copy.46), calls=%async_computation.1 | async-start | bytes 524288 | tf_op jit(solution)/shard_map/all_to_all | solution.py:61
where the time goes:
time: 58.3 us; the launch traced here: 57.7 us
  waiting for transfers between devices  20.6 us (35%)
  starting transfers between devices  16.6 us (28%)
  blocking collectives  8.24 us (14%)
  local copies, waits for them, and re-layouts  6.92 us (12%)
  other arithmetic  5.05 us (9%)
    all_gather x1, blocking collectives, fetch_limit(): band_limit = lax.all_gather(nearest[None, :], 'wide', axis=0, tiled=True)  8.24 us
    all_to_all x1, waiting for transfers between devices, per_device(): lax.all_to_all(send_color, 'grp', split_axis=0, concat_axis=0, tiled=True)  8.05 us
    all_to_all x1, starting transfers between devices, per_device(): lax.all_to_all(send_depth, 'grp', split_axis=0, concat_axis=0, tiled=True)  6.49 us
    all_to_all x1, waiting for transfers between devices, per_device(): lax.all_to_all(accum, 'wide', split_axis=0, concat_axis=0, tiled=True)  5.02 us
    all_to_all x1, waiting for transfers between devices, per_device(): lax.all_to_all(send_depth, 'grp', split_axis=0, concat_axis=0, tiled=True)  4.06 us
    all_to_all x1, waiting for transfers between devices, per_device(): lax.all_to_all(trans, 'wide', split_axis=0, concat_axis=0, tiled=True)  3.43 us
    all_to_all x1, starting transfers between devices, per_device(): lax.all_to_all(send_color, 'grp', split_axis=0, concat_axis=0, tiled=True)  3.41 us
    all_to_all x1, starting transfers between devices, per_device(): lax.all_to_all(accum, 'wide', split_axis=0, concat_axis=0, tiled=True)  3.4 us
  transfers between devices with their start and end apart: 4, of which 4 were waited for; matrix products, arithmetic and copies ran while one was open for 10% of the time, Pallas kernels for 0%

commit v1 on v0

v1 whole, which is shorter than its diff:
```python
import functools

import jax
import jax.numpy as jnp
from jax import lax
from jax.experimental import pallas as pl
from jax.experimental.pallas import tpu as pltpu
from jax.sharding import PartitionSpec as P

TILE_H = 64
TILE_W = 64
SBOX_ROWS = 16
VBOX_ROWS = 32
LANES = 128

far_depth = 1073741824
MESH_ID = pl.DeviceIdType.MESH

NG = TILE_H * TILE_W // LANES
SG = SBOX_ROWS * TILE_W // LANES + 1
VG = VBOX_ROWS * TILE_W // LANES + 1
SPAD = NG - SG
VPAD = NG - VG


def group_of(top, pad):
    return jnp.minimum(lax.div(top * TILE_W, LANES), pad)


def window_inside(box, row, group, groups):
    top, bottom, left, right = [box(row, i) for i in range(4)]
    shape = (groups, 1, LANES)
    lane = lax.broadcasted_iota(jnp.int32, shape, 2)
    pix = lane + (lax.broadcasted_iota(jnp.int32, shape, 0) + group) * LANES
    col = lane & (TILE_W - 1)
    inside = (pix >= top * TILE_W) & (pix < bottom * TILE_W)
    return inside & (col >= left) & (col < right)


def groups_of(load, start, count):
    return jnp.stack([load(start + j) for j in range(count)])


def kernel(
    nw, ng, sbox_t, vbox, order, sbox_v, vbox_v, sdepth, scolor, vcolor, valpha, rentry, rstep,
    out,
    depth_in, scolor_in, color_in, alpha_in, entry_in, step_in,
    sbox_r, vbox_r, sbox_m, vbox_m, dsend, drecv, csend, crecv, winner, surface, vsend, vrecv,
    load_sem, sb_s, sb_r, vb_s, vb_r, d_s, d_r, c_s, c_r, l_s, l_r, v_s, v_r, *limits,
):
    w = lax.axis_index("wide")
    g = lax.axis_index("grp")
    samples = alpha_in.shape[2]

    def sbox(r, i):
        return sbox_t[i, r]

    def vbox_at(c, i):
        return vbox[c, i]

    loads = [
        pltpu.make_async_copy(src, dst, load_sem.at[i])
        for i, (src, dst) in enumerate(
            [(sdepth, depth_in), (scolor, scolor_in), (valpha, alpha_in), (rentry, entry_in), (rstep, step_in), (vcolor, color_in)]
        )
    ]
    loads[0].start()

    barrier = pltpu.get_barrier_semaphore()
    for i in range(1, ng):
        pl.semaphore_signal(barrier, inc=1, device_id=(w, lax.rem(g + i, ng)), device_id_type=MESH_ID)
    for i in range(1, nw):
        pl.semaphore_signal(barrier, inc=1, device_id=(lax.rem(w + i, nw), g), device_id_type=MESH_ID)
    for copy in loads[1:]:
        copy.start()

    loads[0].wait()
    for r in range(ng):
        start = group_of(sbox(r, 0), SPAD)
        inside = window_inside(sbox, r, start, SG)
        depth = groups_of(lambda j: depth_in[j, r : r + 1], start, SG)
        dsend[r] = jnp.where(inside, depth, far_depth)

    pl.semaphore_wait(barrier, ng - 1 + nw - 1)

    def remote(src, dst, send, recv, device):
        return pltpu.make_async_remote_copy(
            src_ref=src, dst_ref=dst, send_sem=send, recv_sem=recv, device_id=device, device_id_type=MESH_ID
        )

    sends = []
    dcopies, ccopies, scopies, vbcopies = [], [], [], []
    for i in range(1, ng):
        peer = lax.rem(g + i, ng)
        scopies.append(remote(sbox_v, sbox_r.at[g], sb_s.at[i], sb_r.at[i], (w, peer)))
        scopies[-1].start()
        dcopies.append(
            remote(
                dsend.at[peer], drecv.at[g, pl.ds(SPAD, SG)], d_s.at[i], d_r.at[i], (w, peer)
            )
        )
        dcopies[-1].start()
    for i in range(1, nw):
        peer = lax.rem(w + i, nw)
        vbcopies.append(remote(vbox_v, vbox_r.at[w], vb_s.at[i], vb_r.at[i], (peer, g)))
        vbcopies[-1].start()
    loads[1].wait()
    for r in range(ng):
        start = group_of(sbox(r, 0), SPAD)
        for ch in range(3):
            color = groups_of(lambda j: scolor_in[ch, j].astype(jnp.float32)[r : r + 1], start, SG)
            csend[r, :, ch : ch + 1] = color
    middle = pl.ds(SPAD, SG)
    for i in range(1, ng):
        peer = lax.rem(g + i, ng)
        ccopies.append(remote(csend.at[peer], crecv.at[g, middle], c_s.at[i], c_r.at[i], (w, peer)))
        ccopies[-1].start()
    crecv[g, middle] = csend[g]

    sbox_r[g] = sbox_v[...]
    vbox_r[w] = vbox_v[...]
    drecv[g, middle] = dsend[g]
    for s in range(ng):
        drecv[s, :SPAD] = jnp.full((SPAD, 1, LANES), far_depth, jnp.int32)
        drecv[s, SPAD + SG :] = jnp.full((SPAD, 1, LANES), far_depth, jnp.int32)
    pad_row = lax.broadcasted_iota(jnp.int32, (VPAD, 4, LANES), 1)
    pad = jnp.where(pad_row == 3, 1.0, 0.0)
    for b in range(nw):
        vrecv[b, :VPAD] = pad
        vrecv[b, VPAD + VG :] = pad

    for copy in scopies:
        copy.wait_recv()
    to_smem = pltpu.make_async_copy(sbox_r, sbox_m, load_sem.at[6])
    to_smem.start()
    to_smem.wait()
    starts = [SPAD - group_of(sbox_m[s, 0, g], SPAD) for s in range(ng)]
    for copy in dcopies:
        copy.wait_recv()
    step = NG // 4

    for q in range(4):
        best = groups_of(lambda j: drecv[0, j], starts[0] + q * step, step)
        win = jnp.zeros_like(best)
        for s in range(1, ng):
            depth = groups_of(lambda j: drecv[s, j], starts[s] + q * step, step)
            win = jnp.where(depth < best, s, win)
            best = jnp.minimum(depth, best)
        limits[0][q * step : (q + 1) * step] = best
        winner[q * step : (q + 1) * step] = jnp.where(best < far_depth, win, -1)

    lcopies = []
    for i in range(1, nw):
        lcopies.append(remote(limits[0], limits[i], l_s.at[i], l_r.at[i], (lax.rem(w + i, nw), g)))
        lcopies[-1].start()
    for copy in loads[2:]:
        copy.wait()

    k_ids = lax.broadcasted_iota(jnp.int32, (VG, samples, LANES), 1)

    def integrate(c, limit):
        start = group_of(vbox[c, 0], VPAD)
        inside = window_inside(vbox_at, c, start, VG)
        bound = jnp.where(inside, groups_of(lambda j: limit[j], start, VG), -1)
        entry = groups_of(lambda j: entry_in[j, pl.ds(c, 1)], start, VG)
        stride = groups_of(lambda j: step_in[j, pl.ds(c, 1)], start, VG)
        kept = entry + k_ids * stride < bound
        alpha = groups_of(lambda j: alpha_in[c, j].astype(jnp.float32), start, VG)
        opacity = jnp.where(kept, alpha, 0.0)
        clear = 1.0 - opacity
        before = jnp.where(k_ids >= 1, pltpu.roll(clear, 1, 1), 1.0)
        shift = 1
        while shift < samples:
            before = before * jnp.where(k_ids >= shift, pltpu.roll(before, shift, 1), 1.0)
            shift *= 2
        weight = opacity * before
        accum = []
        for ch in range(3):
            color = groups_of(lambda j: color_in[c, ch, j].astype(jnp.float32), start, VG)
            accum.append(jnp.sum(weight * color, axis=1, keepdims=True))
        return accum, (before * clear)[:, samples - 1 : samples]

    accum, trans = integrate(w, limits[0])
    window = pl.ds(VPAD, VG)
    for ch in range(3):
        vrecv[w, window, ch : ch + 1] = accum[ch]
    vrecv[w, window, 3:4] = trans

    def vcopy(i):
        c = lax.rem(w + nw - i, nw)
        return remote(vsend.at[c], vrecv.at[w, window], v_s.at[i], v_r.at[i], (c, g))

    for i in range(1, nw):
        c = lax.rem(w + nw - i, nw)
        lcopies[i - 1].wait_recv()
        accum, trans = integrate(c, limits[i])
        for ch in range(3):
            vsend[c, :, ch : ch + 1] = accum[ch]
        vsend[c, :, 3:4] = trans
        vcopy(i).start()

    for copy in ccopies:
        copy.wait_recv()
    for q in range(4):
        win = winner[q * step : (q + 1) * step]
        color = jnp.zeros((step, 3, LANES), jnp.float32)
        for s in range(ng):
            color = jnp.where(win == s, groups_of(lambda j: crecv[s, j], starts[s] + q * step, step), color)
        surface[q * step : (q + 1) * step] = color

    for copy in vbcopies:
        copy.wait_recv()
    to_smem = pltpu.make_async_copy(vbox_r, vbox_m, load_sem.at[7])
    to_smem.start()
    to_smem.wait()
    ranks = [order[0, j] for j in range(nw)]
    offsets = [VPAD - group_of(vbox_m[b, w, 0], VPAD) for b in ranks]
    for i in range(1, nw):
        vcopy(i).wait_recv()
    for q in range(4):
        color = jnp.zeros((step, 3, LANES), jnp.float32)
        through = jnp.ones((step, 1, LANES), jnp.float32)
        for j in range(nw):
            layer = groups_of(lambda i: vrecv[ranks[j], i], offsets[j] + q * step, step)
            color = color + through * layer[:, 0:3]
            through = through * layer[:, 3:4]
        color = color + through * surface[q * step : (q + 1) * step]
        for j in range(step):
            at = slice((q * step + j) * LANES, (q * step + j + 1) * LANES)
            out[0:3, at] = color[j]
            out[3:4, at] = through[j]

    for copy in scopies + dcopies + vbcopies + ccopies + lcopies:
        copy.wait_send()
    for i in range(1, nw):
        vcopy(i).wait_send()


def solution(mesh):
    nw, ng = mesh.shape["wide"], mesh.shape["grp"]

    def per_device(sdepth, scolor, sbox, vcolor, valpha, vbox, rentry, rstep, order):
        sdepth, scolor, sbox = sdepth[0, 0], scolor[0, 0].transpose(1, 0, 2), sbox[0, 0].T
        vcolor, valpha, vbox = vcolor[0, 0].transpose(0, 2, 1, 3), valpha[0, 0], vbox[0, 0]
        rentry, rstep = rentry[0, 0], rstep[0, 0]
        pix = TILE_H * TILE_W

        def grouped(x):
            x = x.reshape(x.shape[:-1] + (NG, LANES))
            return jnp.moveaxis(x, -2, -3)

        sdepth, scolor, vcolor, valpha = grouped(sdepth), grouped(scolor), grouped(vcolor), grouped(valpha)
        rentry, rstep = grouped(rentry), grouped(rstep)
        smem = pl.BlockSpec(memory_space=pltpu.SMEM)
        vmem = pl.BlockSpec(memory_space=pltpu.VMEM)
        hbm = pl.BlockSpec(memory_space=pl.ANY)
        dma = pltpu.SemaphoreType.DMA
        frame = pl.pallas_call(
            functools.partial(kernel, nw, ng),
            out_shape=jax.ShapeDtypeStruct((4, pix), jnp.float32),
            in_specs=[smem] * 3 + [vmem] * 2 + [hbm] * 6,
            out_specs=vmem,
            scratch_shapes=[
                pltpu.VMEM(sdepth.shape, jnp.int32),
                pltpu.VMEM(scolor.shape, jnp.bfloat16),
                pltpu.VMEM(vcolor.shape, jnp.bfloat16),
                pltpu.VMEM(valpha.shape, jnp.bfloat16),
                pltpu.VMEM(rentry.shape, jnp.int32),
                pltpu.VMEM(rstep.shape, jnp.int32),
                pltpu.VMEM((ng,) + sbox.shape, jnp.int32),
                pltpu.VMEM((nw,) + vbox.shape, jnp.int32),
                pltpu.SMEM((ng,) + sbox.shape, jnp.int32),
                pltpu.SMEM((nw,) + vbox.shape, jnp.int32),
                pltpu.VMEM((ng, SG, 1, LANES), jnp.int32),
                pltpu.VMEM((ng, NG + SPAD, 1, LANES), jnp.int32),
                pltpu.VMEM((ng, SG, 3, LANES), jnp.float32),
                pltpu.VMEM((ng, NG + SPAD, 3, LANES), jnp.float32),
                pltpu.VMEM((NG, 1, LANES), jnp.int32),
                pltpu.VMEM((NG, 3, LANES), jnp.float32),
                pltpu.VMEM((nw, VG, 4, LANES), jnp.float32),
                pltpu.VMEM((nw, NG + VPAD, 4, LANES), jnp.float32),
                dma((8,)),
                dma((ng,)), dma((ng,)), dma((nw,)), dma((nw,)),
                dma((ng,)), dma((ng,)), dma((ng,)), dma((ng,)),
                dma((nw,)), dma((nw,)), dma((nw,)), dma((nw,)),
                *[pltpu.VMEM((NG, 1, LANES), jnp.int32)] * nw,
            ],
            compiler_params=pltpu.CompilerParams(collective_id=0, has_side_effects=True),
        )(sbox, vbox, order, sbox, vbox, sdepth, scolor, vcolor, valpha, rentry, rstep)
        return frame[None, None]

    return jax.shard_map(
        per_device,
        mesh=mesh,
        in_specs=(
            P("wide", "grp", None, None),
            P("wide", "grp", None, None, None),
            P("wide", "grp", None, None),
            P("wide", "grp", None, None, None, None),
            P("wide", "grp", None, None, None),
            P("wide", "grp", None, None),
            P("wide", "grp", None, None),
            P("wide", "grp", None, None),
            P("grp", None),
        ),
        out_specs=P("grp", "wide", None, None),
        check_vma=False,
    )
```

time: 58.3 us -> 21 us (0.36)
  waiting for transfers between devices: 20.6 us -> 0 us
  Pallas kernels: 0 us -> 19.3 us
  starting transfers between devices: 16.6 us -> 0 us
  blocking collectives: 8.24 us -> 0 us
  local copies, waits for them, and re-layouts: 6.92 us -> 1.47 us
  other arithmetic: 5.05 us -> 0 us
    all_to_all x4 -> x0, waiting for transfers between devices: 20.6 us -> none  [the longest x1 8.05 us: per_device(): lax.all_to_all(send_color, 'grp', split_axis=0, concat_axis=0, tiled=True)]
    pallas_call x0 -> x1, Pallas kernels: none -> 19.3 us  [per_device(): pl.pallas_call(functools.partial(kernel, nw, ng), out_shape=jax.ShapeDtyp...]
    all_to_all x4 -> x0, starting transfers between devices: 16.6 us -> none  [the longest x1 6.49 us: per_device(): lax.all_to_all(send_depth, 'grp', split_axis=0, concat_axis=0, tiled=True)]
    all_gather x1 -> x0, blocking collectives: 8.24 us -> none  [fetch_limit(): band_limit = lax.all_gather(nearest[None, :], 'wide', axis=0, tiled=True)]
    select_n x7 -> x0, other arithmetic: 1.46 us -> none  [the longest x1 1 us: per_device(): jnp.where(s_inside[:, None, :], color, jnp.zeros((), jnp.bfloat16))]
    gather x2 -> x0, local copies, waits for them, and re-layouts: 1.28 us -> none  [the longest x1 0.7 us: per_device(): ordered_accum = jnp.take(layer_accum, rank, axis=0)]
    slice x2 -> x0, local copies, waits for them, and re-layouts: 1.05 us -> none  [window_mask(): box[..., 0, None, None]]
    add x1 -> x0, local copies, waits for them, and re-layouts: 0.84 us -> none  [per_device(): accum = accum + weight[:, None, :] * vcolor[:, k].astype(jnp.float32)]
  transfers between devices with their start and end apart: 4 -> 0, of which waited for: 4 -> 0; matrix products, arithmetic and copies ran while one was open for 10% -> 0% of each run, Pallas kernels for 0% -> 0%
where the time goes in v1:
time: 21 us; the launch traced here: 20.8 us
  Pallas kernels  19.3 us (92%)
  local copies, waits for them, and re-layouts  1.47 us (7%)
    pallas_call x1, Pallas kernels, per_device(): pl.pallas_call(functools.partial(kernel, nw, ng), out_shape=jax.ShapeDtyp...  19.3 us
    unnamed x1, local copies, waits for them, and re-layouts  1.47 us

profile of v1, /device:TPU:0, one launch (start us, length us, event | category | flops | bytes accessed | tf_op | source)
XLA Modules:
  0.0 20.8 jit_solution(5036715683183005931)
XLA Ops:
  0.0 19.3 %shard_map.91 = f32[4,4096]{1,0:T(4,128)} custom-call(s32[4,8]{1,0:T(4,128)} %bitcast.38, s32[4,4]{1,0:T(4,128)} %bitcast.40, s32[1,4]{1,0:T(1,128)} %order.1, s32[4,8]{1,0:T(4,128)} %bitcast.39, s32[4,4]{1,0:T(4,128)} %bitcast.41, s32[32,8,128]{2,1,0:T(8,128)} %bitcast.35, bf16[3,32,8,128]{3,2,1,0:T(8,128)(2,1)} %bitcast.34, ...), custom_call_target="tpu_custom_call" | custom-call | tf_op jit(solution)/shard_map/pallas_call | solution.py:258
  19.3 1.5 %copy.11 = f32[1,1,4,4096]{3,2,1,0:T(4,128)} copy(f32[1,1,4,4096]{3,2,1,0:T(4,128)} %bitcast.32) | data formatting | bytes 131072

commit v2 on v1

--- a/solution.py
+++ b/solution.py
@@ -42,10 +42,10 @@
 
 
 def kernel(
-    nw, ng, sbox_t, vbox, order, sbox_v, vbox_v, sdepth, scolor, vcolor, valpha, rentry, rstep,
+    nw, ng, sbox_h, vbox_h, order_h, sdepth, scolor, vcolor, valpha, rentry, rstep,
     out,
     depth_in, scolor_in, color_in, alpha_in, entry_in, step_in,
-    sbox_r, vbox_r, sbox_m, vbox_m, dsend, drecv, csend, crecv, winner, surface, vsend, vrecv,
+    sbox_t, vbox, order, sbox_v, vbox_v, box_sem, sbox_r, vbox_r, sbox_m, vbox_m, dsend, drecv, csend, crecv, winner, surface, vsend, vrecv,
     load_sem, sb_s, sb_r, vb_s, vb_r, d_s, d_r, c_s, c_r, l_s, l_r, v_s, v_r, *limits,
 ):
     w = lax.axis_index("wide")
@@ -64,16 +64,25 @@
             [(sdepth, depth_in), (scolor, scolor_in), (valpha, alpha_in), (rentry, entry_in), (rstep, step_in), (vcolor, color_in)]
         )
     ]
-    loads[0].start()
+    smalls = [
+        pltpu.make_async_copy(src, dst, box_sem.at[i])
+        for i, (src, dst) in enumerate(
+            [(sbox_h, sbox_t), (sbox_h, sbox_v), (vbox_h, vbox_v), (vbox_h, vbox), (order_h, order)]
+        )
+    ]
 
     barrier = pltpu.get_barrier_semaphore()
     for i in range(1, ng):
         pl.semaphore_signal(barrier, inc=1, device_id=(w, lax.rem(g + i, ng)), device_id_type=MESH_ID)
     for i in range(1, nw):
         pl.semaphore_signal(barrier, inc=1, device_id=(lax.rem(w + i, nw), g), device_id_type=MESH_ID)
+    loads[0].start()
+    for copy in smalls:
+        copy.start()
     for copy in loads[1:]:
         copy.start()
 
+    smalls[0].wait()
     loads[0].wait()
     for r in range(ng):
         start = group_of(sbox(r, 0), SPAD)
@@ -81,6 +90,8 @@
         depth = groups_of(lambda j: depth_in[j, r : r + 1], start, SG)
         dsend[r] = jnp.where(inside, depth, far_depth)
 
+    for copy in smalls[1:]:
+        copy.wait()
     pl.semaphore_wait(barrier, ng - 1 + nw - 1)
 
     def remote(src, dst, send, recv, device):
@@ -94,6 +105,8 @@
         peer = lax.rem(g + i, ng)
         scopies.append(remote(sbox_v, sbox_r.at[g], sb_s.at[i], sb_r.at[i], (w, peer)))
         scopies[-1].start()
+    for i in range(1, ng):
+        peer = lax.rem(g + i, ng)
         dcopies.append(
             remote(
                 dsend.at[peer], drecv.at[g, pl.ds(SPAD, SG)], d_s.at[i], d_r.at[i], (w, peer)
@@ -251,14 +264,13 @@
 
         sdepth, scolor, vcolor, valpha = grouped(sdepth), grouped(scolor), grouped(vcolor), grouped(valpha)
         rentry, rstep = grouped(rentry), grouped(rstep)
-        smem = pl.BlockSpec(memory_space=pltpu.SMEM)
         vmem = pl.BlockSpec(memory_space=pltpu.VMEM)
         hbm = pl.BlockSpec(memory_space=pl.ANY)
         dma = pltpu.SemaphoreType.DMA
         frame = pl.pallas_call(
             functools.partial(kernel, nw, ng),
             out_shape=jax.ShapeDtypeStruct((4, pix), jnp.float32),
-            in_specs=[smem] * 3 + [vmem] * 2 + [hbm] * 6,
+            in_specs=[hbm] * 9,
             out_specs=vmem,
             scratch_shapes=[
                 pltpu.VMEM(sdepth.shape, jnp.int32),
@@ -267,6 +279,12 @@
                 pltpu.VMEM(valpha.shape, jnp.bfloat16),
                 pltpu.VMEM(rentry.shape, jnp.int32),
                 pltpu.VMEM(rstep.shape, jnp.int32),
+                pltpu.SMEM(sbox.shape, jnp.int32),
+                pltpu.SMEM(vbox.shape, jnp.int32),
+                pltpu.SMEM(order.shape, jnp.int32),
+                pltpu.VMEM(sbox.shape, jnp.int32),
+                pltpu.VMEM(vbox.shape, jnp.int32),
+                dma((5,)),
                 pltpu.VMEM((ng,) + sbox.shape, jnp.int32),
                 pltpu.VMEM((nw,) + vbox.shape, jnp.int32),
                 pltpu.SMEM((ng,) + sbox.shape, jnp.int32),
@@ -286,7 +304,7 @@
                 *[pltpu.VMEM((NG, 1, LANES), jnp.int32)] * nw,
             ],
             compiler_params=pltpu.CompilerParams(collective_id=0, has_side_effects=True),
-        )(sbox, vbox, order, sbox, vbox, sdepth, scolor, vcolor, valpha, rentry, rstep)
+        )(sbox, vbox, order, sdepth, scolor, vcolor, valpha, rentry, rstep)
         return frame[None, None]
 
     return jax.shard_map(

time: 21 us -> 20.2 us (0.962)
  Pallas kernels: 19.3 us -> 18.5 us
    pallas_call x1, Pallas kernels: 19.3 us -> 18.5 us  [per_device(): pl.pallas_call(functools.partial(kernel, nw, ng), out_shape=jax.ShapeDtyp...]
where the time goes in v2:
time: 20.2 us; the launch traced here: 20 us
  Pallas kernels  18.5 us (92%)
  local copies, waits for them, and re-layouts  1.47 us (7%)
    pallas_call x1, Pallas kernels, per_device(): pl.pallas_call(functools.partial(kernel, nw, ng), out_shape=jax.ShapeDtyp...  18.5 us
    unnamed x1, local copies, waits for them, and re-layouts  1.47 us

profile of v2, /device:TPU:0, one launch (start us, length us, event | category | flops | bytes accessed | tf_op | source)
XLA Modules:
  0.0 20.0 jit_solution(17839228445694834979)
XLA Ops:
  0.0 18.5 %shard_map.91 = f32[4,4096]{1,0:T(4,128)} custom-call(s32[4,8]{1,0:T(4,128)} %bitcast.38, s32[4,4]{1,0:T(4,128)} %bitcast.39, s32[1,4]{1,0:T(1,128)} %order_h.1, s32[32,8,128]{2,1,0:T(8,128)} %bitcast.35, bf16[3,32,8,128]{3,2,1,0:T(8,128)(2,1)} %bitcast.34, bf16[4,3,32,8,128]{4,3,2,1,0:T(8,128)(2,1)} %bitcast.31, bf16[4,32,8,128]{3,2,1,0:T(8,128)(2,1)} %bitcast.33, ...), custom_call_target="tpu_custom_call" | custom-call | tf_op jit(solution)/shard_map/pallas_call | solution.py:270
  18.5 1.5 %copy.11 = f32[1,1,4,4096]{3,2,1,0:T(4,128)} copy(f32[1,1,4,4096]{3,2,1,0:T(4,128)} %bitcast.32) | data formatting | bytes 131072

commit v3 on v2

--- a/solution.py
+++ b/solution.py
@@ -14,6 +14,9 @@
 LANES = 128
 
 far_depth = 1073741824
+ALPHA_MAX = 0.039794922
+COLOR_MAX = 4.0
+HALF = 32767.0
 MESH_ID = pl.DeviceIdType.MESH
 
 NG = TILE_H * TILE_W // LANES
@@ -45,7 +48,7 @@
     nw, ng, sbox_h, vbox_h, order_h, sdepth, scolor, vcolor, valpha, rentry, rstep,
     out,
     depth_in, scolor_in, color_in, alpha_in, entry_in, step_in,
-    sbox_t, vbox, order, sbox_v, vbox_v, box_sem, sbox_r, vbox_r, sbox_m, vbox_m, dsend, drecv, csend, crecv, winner, surface, vsend, vrecv,
+    sbox_t, vbox, order, sbox_v, vbox_v, box_sem, sbox_r, vbox_r, sbox_m, vbox_m, dsend, drecv, csend, crecv, winner, surface, seg, vsend, vrecv,
     load_sem, sb_s, sb_r, vb_s, vb_r, d_s, d_r, c_s, c_r, l_s, l_r, v_s, v_r, *limits,
 ):
     w = lax.axis_index("wide")
@@ -136,8 +139,8 @@
     for s in range(ng):
         drecv[s, :SPAD] = jnp.full((SPAD, 1, LANES), far_depth, jnp.int32)
         drecv[s, SPAD + SG :] = jnp.full((SPAD, 1, LANES), far_depth, jnp.int32)
-    pad_row = lax.broadcasted_iota(jnp.int32, (VPAD, 4, LANES), 1)
-    pad = jnp.where(pad_row == 3, 1.0, 0.0)
+    most = 1.001 * (1.0 - (1.0 - ALPHA_MAX) ** samples)
+    pad = jnp.full((VPAD, 4, LANES), -HALF, jnp.float32).astype(jnp.int32).astype(jnp.int16)
     for b in range(nw):
         vrecv[b, :VPAD] = pad
         vrecv[b, VPAD + VG :] = pad
@@ -195,21 +198,24 @@
 
     accum, trans = integrate(w, limits[0])
     window = pl.ds(VPAD, VG)
-    for ch in range(3):
-        vrecv[w, window, ch : ch + 1] = accum[ch]
-    vrecv[w, window, 3:4] = trans
+
+    def coded(accum, trans):
+        for ch in range(3):
+            seg[:, ch : ch + 1] = accum[ch] * (2.0 * HALF / (most * COLOR_MAX)) - HALF
+        seg[:, 3:4] = (1.0 - trans) * (2.0 * HALF / most) - HALF
+        return jnp.round(seg[...]).astype(jnp.int32).astype(jnp.int16)
+
+    vrecv[w, window] = coded(accum, trans)
 
     def vcopy(i):
         c = lax.rem(w + nw - i, nw)
         return remote(vsend.at[c], vrecv.at[w, window], v_s.at[i], v_r.at[i], (c, g))
 
-    for i in range(1, nw):
+    for i in sorted(range(1, nw), key=lambda i: abs(i - nw // 2)):
         c = lax.rem(w + nw - i, nw)
         lcopies[i - 1].wait_recv()
         accum, trans = integrate(c, limits[i])
-        for ch in range(3):
-            vsend[c, :, ch : ch + 1] = accum[ch]
-        vsend[c, :, 3:4] = trans
+        vsend[c] = coded(accum, trans)
         vcopy(i).start()
 
     for copy in ccopies:
@@ -234,9 +240,12 @@
         color = jnp.zeros((step, 3, LANES), jnp.float32)
         through = jnp.ones((step, 1, LANES), jnp.float32)
         for j in range(nw):
-            layer = groups_of(lambda i: vrecv[ranks[j], i], offsets[j] + q * step, step)
-            color = color + through * layer[:, 0:3]
-            through = through * layer[:, 3:4]
+            layer = groups_of(
+                lambda i: vrecv[ranks[j], i].astype(jnp.int32).astype(jnp.float32), offsets[j] + q * step, step
+            )
+            layer = (layer + HALF) * (most / (2.0 * HALF))
+            color = color + through * (layer[:, 0:3] * COLOR_MAX)
+            through = through * (1.0 - layer[:, 3:4])
         color = color + through * surface[q * step : (q + 1) * step]
         for j in range(step):
             at = slice((q * step + j) * LANES, (q * step + j + 1) * LANES)
@@ -295,8 +304,9 @@
                 pltpu.VMEM((ng, NG + SPAD, 3, LANES), jnp.float32),
                 pltpu.VMEM((NG, 1, LANES), jnp.int32),
                 pltpu.VMEM((NG, 3, LANES), jnp.float32),
-                pltpu.VMEM((nw, VG, 4, LANES), jnp.float32),
-                pltpu.VMEM((nw, NG + VPAD, 4, LANES), jnp.float32),
+                pltpu.VMEM((VG, 4, LANES), jnp.float32),
+                pltpu.VMEM((nw, VG, 4, LANES), jnp.int16),
+                pltpu.VMEM((nw, NG + VPAD, 4, LANES), jnp.int16),
                 dma((8,)),
                 dma((ng,)), dma((ng,)), dma((nw,)), dma((nw,)),
                 dma((ng,)), dma((ng,)), dma((ng,)), dma((ng,)),

time: 20.2 us -> 20.1 us (level)
  no operation moved by 1% of the time
where the time goes in v3:
time: 20.1 us; the launch traced here: 19.9 us
  Pallas kernels  18.4 us (92%)
  local copies, waits for them, and re-layouts  1.47 us (7%)
    pallas_call x1, Pallas kernels, per_device(): pl.pallas_call(functools.partial(kernel, nw, ng), out_shape=jax.ShapeDtyp...  18.4 us
    unnamed x1, local copies, waits for them, and re-layouts  1.47 us

profile of v3, /device:TPU:0, one launch (start us, length us, event | category | flops | bytes accessed | tf_op | source)
XLA Modules:
  0.0 19.9 jit_solution(3124509158384972443)
XLA Ops:
  0.0 18.4 %shard_map.91 = f32[4,4096]{1,0:T(4,128)} custom-call(s32[4,8]{1,0:T(4,128)} %bitcast.38, s32[4,4]{1,0:T(4,128)} %bitcast.39, s32[1,4]{1,0:T(1,128)} %order_h.1, s32[32,8,128]{2,1,0:T(8,128)} %bitcast.35, bf16[3,32,8,128]{3,2,1,0:T(8,128)(2,1)} %bitcast.34, bf16[4,3,32,8,128]{4,3,2,1,0:T(8,128)(2,1)} %bitcast.31, bf16[4,32,8,128]{3,2,1,0:T(8,128)(2,1)} %bitcast.33, ...), custom_call_target="tpu_custom_call" | custom-call | tf_op jit(solution)/shard_map/pallas_call | solution.py:279
  18.4 1.5 %copy.11 = f32[1,1,4,4096]{3,2,1,0:T(4,128)} copy(f32[1,1,4,4096]{3,2,1,0:T(4,128)} %bitcast.32) | data formatting | bytes 131072
